TPU v7x, 32 devices: a whole 2x2x4 slice. The times are simulated.
32 devices in a mesh: gx: 4 (over z), gy: 4 (over x, core), gz: 2 (over y).
Axes of the slice: x: 2, y: 2, z: 4, core: 2. Of those that a mesh axis runs over, the one named last changes fastest.
Arguments:
- inputs: bfloat16 [112, 112, 14, 96], P('gx', 'gy', 'gz'), may hold values from -6 to 6
- d_out: bfloat16 [112, 112, 14, 96], P('gx', 'gy', 'gz'), may hold values from -6 to 6
- layer_norm_gain: float32 [96], replicated, may hold values from 0.1 to 1.9
- layer_norm_bias: float32 [96], replicated, may hold values from -3 to 3
- w_qkv: bfloat16 [96, 288], replicated, may hold values from -0.625 to 0.625
- b_qkv: float32 [288], replicated, may hold values from -3 to 3
- w_proj: bfloat16 [96, 96], replicated, may hold values from -0.625 to 0.625
- rel_bias: float32 [3, 2197], replicated, may hold values from -4 to 240
Outputs:
- d_x: bfloat16 [112, 112, 14, 96], P('gx', 'gy', 'gz')
- g_qkv: float32 [96, 288], replicated
- g_bqkv: float32 [288], replicated
- g_proj: float32 [96, 96], replicated
- g_rel: float32 [3, 2197], replicated
- gain_gradient: float32 [96], replicated
- g_shift: float32 [96], replicated
All inputs are finite; a program needn't handle non-finite values.
Results may differ from a plain program's by a relative error of at most 0.011.
Values may be sent and summed in bfloat16 or wider, within the bound.
No kernel may reach another device: no remote copies, remote signals or barrier semaphores. Data moves between devices by JAX's collectives and lax.ppermute only.
A program may use at most 192 MiB of HBM per device.

v0:
```python
import jax
import jax.numpy as jnp
from jax import lax
from jax.sharding import PartitionSpec as P

WIN = 7
SHIFT = 3


def shifted(block, axis, distance):
    devices = range(lax.axis_size(axis))
    route = [((i - distance) % len(devices), i) for i in devices]
    return lax.ppermute(block, axis, route)


def offset_ones(span):
    first = jnp.arange(span)[:, None, None]
    second = jnp.arange(span)[None, :, None]
    third = jnp.arange(2 * span - 1)[None, None, :]
    return (first - second + span - 1 == third).astype(jnp.float32)


def expand_table(table, span):
    exact = lax.Precision.HIGHEST
    ones = offset_ones(span)
    width = 2 * span - 1
    heads = table.shape[0]
    cube = table.reshape(heads, width, width, width)
    section = jnp.einsum("hxyz,cCz->hxycC", cube, ones, precision=exact)
    section = jnp.einsum("hxycC,bBy->hxbcBC", section, ones, precision=exact)
    section = jnp.einsum("hxbcBC,aAx->habcABC", section, ones, precision=exact)
    return section.reshape(heads, span**3, span**3)


def fold_table(pairs, span):
    exact = lax.Precision.HIGHEST
    ones = offset_ones(span)
    heads = pairs.shape[0]
    grid = pairs.reshape(heads, span, span, span, span, span, span)
    section = jnp.einsum("habcABC,aAx->hxbcBC", grid, ones, precision=exact)
    section = jnp.einsum("hxbcBC,bBy->hxycC", section, ones, precision=exact)
    section = jnp.einsum("hxycC,cCz->hxyz", section, ones, precision=exact)
    return section.reshape(heads, -1)


def region_label(start, cells, count):
    places = start + jnp.arange(cells)
    return jnp.where(places < count - WIN, 0, jnp.where(places < count - SHIFT, 1, 2)).astype(
        jnp.int32
    )


def to_windows(array):
    first, second, third = array.shape[:3]
    rest = array.shape[3:]
    shaped = array.reshape((first // WIN, WIN, second // WIN, WIN, third // WIN, WIN) + rest)
    order = (0, 2, 4, 1, 3, 5) + tuple(range(6, 6 + len(rest)))
    return shaped.transpose(order).reshape((-1, WIN**3) + rest)


def from_windows(array, first, second, third):
    feats = array.shape[-1]
    shaped = array.reshape(first // WIN, second // WIN, third // WIN, WIN, WIN, WIN, feats)
    return shaped.transpose(0, 3, 1, 4, 2, 5, 6).reshape(first, second, third, feats)


def forward_depth(pair):
    arrived = shifted(pair[:, :SHIFT], "gx", -1)
    return jnp.concatenate([pair[:, SHIFT:], arrived], 1)


def forward_height(pair):
    arrived = shifted(pair[:, :, :SHIFT], "gy", -1)
    return jnp.concatenate([pair[:, :, SHIFT:], arrived], 2)


def forward_width(pair):
    arrived = shifted(pair[:, :, :, :SHIFT], "gz", -1)
    return jnp.concatenate([pair[:, :, :, SHIFT:], arrived], 3)


def backward_depth(field):
    edge = field.shape[0] - SHIFT
    arrived = shifted(field[edge:], "gx", 1)
    return jnp.concatenate([arrived, field[:edge]], 0)


def backward_height(field):
    edge = field.shape[1] - SHIFT
    arrived = shifted(field[:, edge:], "gy", 1)
    return jnp.concatenate([arrived, field[:, :edge]], 1)


def backward_width(field):
    edge = field.shape[2] - SHIFT
    arrived = shifted(field[:, :, edge:], "gz", 1)
    return jnp.concatenate([arrived, field[:, :, :edge]], 2)


def window_pass(ln_w, dy_w, lab_w, w_qkv, b_qkv, w_proj, bias_full):
    f32 = jnp.float32
    bf16 = jnp.bfloat16
    group, tok, feats = ln_w.shape
    heads = bias_full.shape[0]
    hdim = feats // heads
    scale = hdim ** (-0.5)
    qkv = jnp.einsum("gtc,cf->gtf", ln_w, w_qkv, preferred_element_type=f32) + b_qkv
    qkv = qkv.astype(bf16).reshape(group, tok, 3, heads, hdim)
    query = qkv[:, :, 0].transpose(0, 2, 1, 3)
    keys = qkv[:, :, 1].transpose(0, 2, 1, 3)
    values = qkv[:, :, 2].transpose(0, 2, 1, 3)
    scores = (
        jnp.einsum("ghid,ghjd->ghij", query, keys, preferred_element_type=f32) * scale
        + bias_full[None]
    )
    allowed = (lab_w[:, :, None] == lab_w[:, None, :])[:, None]
    scores = jnp.where(allowed, scores, f32(-1e30))
    top = jnp.max(scores, -1, keepdims=True)
    expo = jnp.exp(scores - top)
    probs = expo / jnp.sum(expo, -1, keepdims=True)
    probs_b = probs.astype(bf16)
    attended = jnp.einsum("ghij,ghjd->ghid", probs_b, values, preferred_element_type=f32)
    attended = attended.transpose(0, 2, 1, 3).reshape(group, tok, feats).astype(bf16)
    grad_att = jnp.einsum("gtc,fc->gtf", dy_w, w_proj, preferred_element_type=f32).astype(bf16)
    proj_part = jnp.einsum("gtf,gtc->fc", attended, dy_w, preferred_element_type=f32)
    grad_heads = grad_att.reshape(group, tok, heads, hdim).transpose(0, 2, 1, 3)
    grad_probs = jnp.einsum("ghid,ghjd->ghij", grad_heads, values, preferred_element_type=f32)
    grad_v = jnp.einsum("ghij,ghid->ghjd", probs_b, grad_heads, preferred_element_type=f32)
    grad_scores = probs * (grad_probs - jnp.sum(probs * grad_probs, -1, keepdims=True))
    rel_part = jnp.sum(grad_scores, 0)
    scores_b = grad_scores.astype(bf16)
    grad_q = jnp.einsum("ghij,ghjd->ghid", scores_b, keys, preferred_element_type=f32) * scale
    grad_k = jnp.einsum("ghij,ghid->ghjd", scores_b, query, preferred_element_type=f32) * scale
    grad_qkv = (
        jnp.stack([grad_q, grad_k, grad_v], 1)
        .transpose(0, 3, 1, 2, 4)
        .reshape(group, tok, 3 * feats)
    )
    bias_part = jnp.sum(grad_qkv, (0, 1))
    qkv_b = grad_qkv.astype(bf16)
    weight_part = jnp.einsum("gtc,gtf->cf", ln_w, qkv_b, preferred_element_type=f32)
    grad_in = jnp.einsum("gtf,cf->gtc", qkv_b, w_qkv, preferred_element_type=f32)
    return (grad_in, (weight_part, bias_part, proj_part, rel_part))


def shards(inputs, d_out, layer_norm_gain, layer_norm_bias, w_qkv, b_qkv, w_proj, rel_bias):
    f32 = jnp.float32
    cells_x, cells_y, cells_z, feats = inputs.shape
    tok = WIN**3
    heads = rel_bias.shape[0]
    xf = inputs.astype(f32)
    centered_input = xf - jnp.mean(xf, -1, keepdims=True)
    inverse_deviation = lax.rsqrt(
        jnp.mean(centered_input * centered_input, -1, keepdims=True) + 1e-05
    )
    normalized_input = centered_input * inverse_deviation
    normalized_tokens = (normalized_input * layer_norm_gain + layer_norm_bias).astype(jnp.bfloat16)
    moved_pair = jnp.stack([normalized_tokens, d_out])
    forward_steps = (forward_depth, forward_height, forward_width)
    backward_steps = (backward_depth, backward_height, backward_width)
    for advance in forward_steps:
        moved_pair = advance(moved_pair)
    label_x = region_label(lax.axis_index("gx") * cells_x, cells_x, cells_x * lax.axis_size("gx"))
    label_y = region_label(lax.axis_index("gy") * cells_y, cells_y, cells_y * lax.axis_size("gy"))
    label_z = region_label(lax.axis_index("gz") * cells_z, cells_z, cells_z * lax.axis_size("gz"))
    labels = label_x[:, None, None] * 9 + label_y[None, :, None] * 3 + label_z[None, None, :]
    bias_full = expand_table(rel_bias, WIN)
    group = cells_y // WIN * (cells_z // WIN)
    win_ln = to_windows(moved_pair[0]).reshape(-1, group, tok, feats)
    win_dy = to_windows(moved_pair[1]).reshape(-1, group, tok, feats)
    win_lab = to_windows(labels).reshape(-1, group, tok)

    def step(carry, item):
        grad_in, parts = window_pass(item[0], item[1], item[2], w_qkv, b_qkv, w_proj, bias_full)
        return (tuple((total + part for total, part in zip(carry, parts))), grad_in)

    start = (
        jnp.zeros((feats, 3 * feats), f32),
        jnp.zeros((3 * feats,), f32),
        jnp.zeros((feats, feats), f32),
        jnp.zeros((heads, tok, tok), f32),
    )
    sums, grad_win = lax.scan(step, start, (win_ln, win_dy, win_lab))
    normalized_output_gradient = from_windows(
        grad_win.reshape(-1, tok, feats), cells_x, cells_y, cells_z
    )
    for retreat in backward_steps:
        normalized_output_gradient = retreat(normalized_output_gradient)
    normalized_gradient = normalized_output_gradient * layer_norm_gain
    input_gradient_norm = inverse_deviation * (
        normalized_gradient
        - jnp.mean(normalized_gradient, -1, keepdims=True)
        - normalized_input * jnp.mean(normalized_gradient * normalized_input, -1, keepdims=True)
    )
    d_x = (d_out.astype(f32) + input_gradient_norm).astype(jnp.bfloat16)
    rel_local = fold_table(sums[3], WIN)
    local_gain = jnp.sum(normalized_output_gradient * normalized_input, (0, 1, 2))
    shift_local = jnp.sum(normalized_output_gradient, (0, 1, 2))
    totals = lax.psum(
        (sums[0], sums[1], sums[2], rel_local, local_gain, shift_local), ("gx", "gy", "gz")
    )
    count = (
        cells_x
        * cells_y
        * cells_z
        * lax.axis_size("gx")
        * lax.axis_size("gy")
        * lax.axis_size("gz")
    )
    inverse_width_factor = float(count) ** (-0.5)
    return (
        d_x,
        totals[0] * inverse_width_factor,
        totals[1] * inverse_width_factor,
        totals[2] * inverse_width_factor,
        totals[3] * inverse_width_factor,
        totals[4] * inverse_width_factor,
        totals[5] * inverse_width_factor,
    )


def solution(mesh):
    placed = (P("gx", "gy", "gz", None), P("gx", "gy", "gz", None), P(), P(), P(), P(), P(), P())
    return jax.shard_map(
        shards,
        mesh=mesh,
        in_specs=placed,
        out_specs=(P("gx", "gy", "gz", None), P(), P(), P(), P(), P(), P()),
        check_vma=False,
    )
```

profile of v0, /device:TPU:0, one launch (start us, length us, event | category | flops | bytes accessed | tf_op | source)
XLA Modules:
  0.0 697.9 jit_solution(15601233751291478034)
XLA Ops:
  15.1 5.1 collective-permute-start
  21.9 9.5 %convolution_bitcast_fusion.5 = f32[3,13,7,7,7,7]{1,2,5,3,0,4:T(8,128)S(1)} fusion(f32[3,13,13,7,7]{2,3,1,0,4:T(8,128)S(1)} %convolution_bitcast_fusion.7, s32[7,7]{0,1:T(8,128)S(1)} %subtract_add_fusion), kind=kOutput, calls=%fused_computation.96 | convolution fusion | flops 14608321 | bytes 474124 | tf_op jit(solution)/shard_map/hxycC,bBy->hxbcBC/dot_general | solution.py:30
  32.4 18.0 %collective-permute-start.1 = (bf16[2,28,3,7,96]{4,3,2,1,0:T(8,128)(2,1)S(1)}, bf16[2,28,3,7,96]{4,3,2,1,0:T(8,128)(2,1)S(1)}, u32[]{:S(2)}, u32[]{:S(2)}) collective-permute-start(bf16[2,28,3,7,96]{4,3,2,1,0:T(8,128)(2,1)S(1)} %pad_maximum_fusion.5), channel_id=1, source_target_pairs={{2,0},{4,2},{6,4},{0,6},{3,1},{5,3},{7,5},{1,7},{10,8},{12,10},{14... | collective-permute-start | bytes 677384 | tf_op jit(solution)/shard_map/ppermute | solution.py:13
  60.5 71.1 %convolution_bitcast_fusion.3 = f32[3,7,7,7,7,7,7]{6,4,5,3,2,0,1:T(8,128)} fusion(f32[3,13,7,7,7,7]{1,2,5,3,0,4:T(8,128)S(1)} %convolution_bitcast_fusion.5, pred[7,7,13,1,1,1,1]{2,0,1,6,5,4,3:T(8,128)(4,1)S(1)} %fusion.73), kind=kOutput, calls=%fused_computation.61 | convolution fusion | flops 55059736 | bytes 1786981 | tf_op jit(solution)/shard_map/hxbcBC,aAx->habcABC/dot_general | solution.py:31
  131.7 59.5 %copy.82 = f32[3,7,7,7,7,7,7]{3,2,1,6,5,4,0:T(8,128)} copy(f32[3,7,7,7,7,7,7]{6,4,5,3,2,0,1:T(8,128)} %convolution_bitcast_fusion.3) | data formatting | bytes 2823576
  191.2 20.9 %add.240 = f32[3,343,343]{1,2,0:T(8,128)} reshape(f32[3,7,7,7,7,7,7]{3,2,1,6,5,4,0:T(8,128)} %copy.82) | data formatting | bytes 2823576 | tf_op jit(solution)/shard_map/while/body/eval_jaxpr/add | solution.py:113
  228.5 134.0 %while.20 = (s32[]{:T(128)}, f32[96,288]{1,0:T(8,128)}, f32[288]{0:T(512)S(1)}, f32[96,96]{1,0:T(8,128)S(1)}, f32[3,343,343]{1,2,0:T(8,128)}, /*index=5*/f32[4,4...) while((s32[]{:T(128)}, f32[96,288]{1,0:T(8,128)}, ...), condition=%wide.wide.region_8.9_spmd.clone, body=%wide.wide.region_2.8_spmd.clone.sunk | while | flops 848489408 | bytes 107633568 | solution.py:183
  231.1 7.0 fusion.174
  238.3 6.9 multiply_reduce_fusion.4
  263.4 7.0 fusion.174
  270.7 6.9 multiply_reduce_fusion.4
  297.2 7.0 fusion.174
  304.5 6.9 multiply_reduce_fusion.4
  331.0 7.0 fusion.174
  338.3 6.9 multiply_reduce_fusion.4
  368.9 20.0 %reshape.160 = f32[3,7,7,7,7,7,7]{3,2,1,6,5,4,0:T(8,128)} reshape(f32[3,343,343]{1,2,0:T(8,128)S(1)} %copy-done) | data formatting | bytes 2823576 | tf_op jit(solution)/shard_map/reshape | solution.py:39
  388.9 59.6 %copy.88 = f32[3,7,7,7,7,7,7]{1,6,4,5,3,2,0:T(8,128)} copy(f32[3,7,7,7,7,7,7]{3,2,1,6,5,4,0:T(8,128)} %reshape.160) | data formatting | bytes 2823576 | tf_op jit(solution)/shard_map/reshape | solution.py:39
  450.1 25.1 %convolution_bitcast_fusion.4 = f32[3,13,7,7,7,7]{1,5,4,3,2,0:T(8,128)} fusion(f32[3,7,7,7,7,7,7]{1,6,4,5,3,2,0:T(8,128)} %copy.88, s32[7,7]{0,1:T(8,128)S(1)} %copy-done.22), kind=kOutput, calls=%fused_computation.95 | convolution fusion | flops 55060372 | bytes 1786540 | tf_op jit(solution)/shard_map/habcABC,aAx->hxbcBC/dot_general | solution.py:40
  475.2 12.8 %copy.89 = f32[3,13,7,7,7,7]{2,3,4,5,1,0:T(8,128)} copy(f32[3,13,7,7,7,7]{1,5,4,3,2,0:T(8,128)} %convolution_bitcast_fusion.4) | data formatting | bytes 749112 | tf_op jit(solution)/shard_map/habcABC,aAx->hxbcBC/transpose | solution.py:40
  493.0 5.4 convolution_bitcast_fusion.6
  499.7 121.2 %all-reduce.3.cloned.1.call-done = f32[96,288]{1,0:T(8,128)} async-done(((f32[96,288]{1,0:T(8,128)}), f32[96,288]{1,0:T(8,128)}) %all-reduce.3.cloned.1.call-update) | async-done | bytes 110608 | tf_op jit(solution)/shard_map/psum | solution.py:199
  628.2 5.9 fusion.61
  634.2 43.7 %all-reduce = (f32[288]{0:T(512)S(1)}, f32[96,96]{1,0:T(8,128)S(1)}, f32[3,2197]{1,0:T(4,128)S(1)}, f32[96]{0:T(128)S(1)}, f32[96]{0:T(128)S(1)}) all-reduce(f32[288]{0:T(512)S(1)} %get-tuple-element.80, f32[96,96]{1,0:T(8,128)S(1)} %get-tuple-element.81, ...), channel_id=1, replica_groups=mesh['gx'=4,'gy'=4,'gz'=2] {'gx','gy','gz'}, use_global_device_ids=true, to_apply=%region_12.13 | all-reduce | flops 16287 | bytes 130296 | tf_op jit(solution)/shard_map/psum | solution.py:199
  682.9 8.0 %fusion.60 = bf16[28,28,7,96]{3,2,1,0:T(8,128)(2,1)} fusion(bf16[28,28,7,96]{3,2,1,0:T(8,128)(2,1)S(1)} %copy-done.2, bf16[28,28,7,96]{3,2,1,0:T(8,128)(2,1)S(1)} %copy-done.6, f32[28,28,7]{2,1,0:T(8,128)S(1)} %broadcast_multiply_fusion, f32[28,28,7]{2,1,0:T(8,128)S(1)} %broadcast_multiply_fusion.1, f32[96]{0:T(128)S(1)} %copy-done.26, ...), kind=kLoop, calls=%fused_computation.78 | loop fusion | flops 6322176 | bytes 5356672 | tf_op jit(solution)/shard_map/convert_element_type | solution.py:195
  (238 shorter events, 140.9 us)
Async XLA Ops:
  7.2 613.7 %all-reduce.3.cloned.1.call-start = ((), (), s32[]{:S(2)}) async-start(), calls=%async_computation | async-start | bytes 294912 | tf_op jit(solution)/shard_map/psum | solution.py:199
  15.1 17.2 %collective-permute-start = (bf16[2,3,28,7,96]{4,3,2,1,0:T(8,128)(2,1)S(1)}, bf16[2,3,28,7,96]{4,3,2,1,0:T(8,128)(2,1)S(1)}, u32[]{:S(2)}, u32[]{:S(2)}) collective-permute-start(bf16[2,3,28,7,96]{4,3,2,1,0:T(8,128)(2,1)S(1)} %pad_maximum_fusion.6), channel_id=1, source_target_pairs={{8,0},{16,8},{24,16},{0,24},{9,1},{17,9},{25,17},{1,25},{10,2},{18... | collective-permute-start | bytes 677384 | tf_op jit(solution)/shard_map/ppermute | solution.py:13
  20.2 30.2 %copy-start.21 = (s32[7,7]{0,1:T(8,128)}, s32[7,7]{0,1:T(8,128)S(1)}, u32[]{:S(2)}) copy-start(s32[7,7]{0,1:T(8,128)S(1)} %subtract_add_fusion) | copy-start | bytes 592
  20.5 11.0 %copy-start.12 = (bf16[1,28,28,7,96]{4,3,2,1,0:T(8,128)(2,1)S(1)}, bf16[1,28,28,7,96]{4,3,2,1,0:T(8,128)(2,1)}, u32[]{:S(2)}) copy-start(bf16[1,28,28,7,96]{4,3,2,1,0:T(8,128)(2,1)} %copy-done.11) | copy-start | bytes 3161092
  32.4 22.8 %collective-permute-start.1 = (bf16[2,28,3,7,96]{4,3,2,1,0:T(8,128)(2,1)S(1)}, bf16[2,28,3,7,96]{4,3,2,1,0:T(8,128)(2,1)S(1)}, u32[]{:S(2)}, u32[]{:S(2)}) collective-permute-start(bf16[2,28,3,7,96]{4,3,2,1,0:T(8,128)(2,1)S(1)} %pad_maximum_fusion.5), channel_id=1, source_target_pairs={{2,0},{4,2},{6,4},{0,6},{3,1},{5,3},{7,5},{1,7},{10,8},{12,10},{14... | collective-permute-start | bytes 677384 | tf_op jit(solution)/shard_map/ppermute | solution.py:13
  59.0 156.9 %collective-permute-start.2 = (bf16[2,28,28,3,96]{4,0,3,2,1:T(2,128)(2,1)}, bf16[2,28,28,3,96]{4,0,3,2,1:T(2,128)(2,1)}, u32[]{:S(2)}, u32[]{:S(2)}) collective-permute-start(bf16[2,28,28,3,96]{4,0,3,2,1:T(2,128)(2,1)} %copy.74), channel_id=1, source_target_pairs={{1,0},{0,1},{3,2},{2,3},{5,4},{4,5},{7,6},{6,7},{9,8},{8,9},{11,10... | collective-permute-start | bytes 2709512 | tf_op jit(solution)/shard_map/ppermute | solution.py:13
  228.7 9.3 %copy-start.9 = (bf16[4,4,343,96]{2,3,1,0:T(8,128)(2,1)}, bf16[4,4,343,96]{2,3,1,0:T(8,128)(2,1)S(1)}, u32[]{:S(2)}) copy-start(bf16[4,4,343,96]{2,3,1,0:T(8,128)(2,1)S(1)} %get-tuple-element.416) | copy-start | bytes 3161092 | tf_op jit(solution)/shard_map/while
  228.7 9.3 %copy-start.13 = (bf16[4,4,343,96]{2,3,1,0:T(8,128)(2,1)}, bf16[4,4,343,96]{2,3,1,0:T(8,128)(2,1)S(1)}, u32[]{:S(2)}) copy-start(bf16[4,4,343,96]{2,3,1,0:T(8,128)(2,1)S(1)} %get-tuple-element.421) | copy-start | bytes 3161092 | tf_op jit(solution)/shard_map/while
  238.3 6.9 slice-start
  261.1 9.3 %copy-start.9 = (bf16[4,4,343,96]{2,3,1,0:T(8,128)(2,1)}, bf16[4,4,343,96]{2,3,1,0:T(8,128)(2,1)S(1)}, u32[]{:S(2)}) copy-start(bf16[4,4,343,96]{2,3,1,0:T(8,128)(2,1)S(1)} %get-tuple-element.416) | copy-start | bytes 3161092 | tf_op jit(solution)/shard_map/while
  261.1 9.3 %copy-start.13 = (bf16[4,4,343,96]{2,3,1,0:T(8,128)(2,1)}, bf16[4,4,343,96]{2,3,1,0:T(8,128)(2,1)S(1)}, u32[]{:S(2)}) copy-start(bf16[4,4,343,96]{2,3,1,0:T(8,128)(2,1)S(1)} %get-tuple-element.421) | copy-start | bytes 3161092 | tf_op jit(solution)/shard_map/while
  270.7 6.9 slice-start
  294.9 9.3 %copy-start.9 = (bf16[4,4,343,96]{2,3,1,0:T(8,128)(2,1)}, bf16[4,4,343,96]{2,3,1,0:T(8,128)(2,1)S(1)}, u32[]{:S(2)}) copy-start(bf16[4,4,343,96]{2,3,1,0:T(8,128)(2,1)S(1)} %get-tuple-element.416) | copy-start | bytes 3161092 | tf_op jit(solution)/shard_map/while
  294.9 9.3 %copy-start.13 = (bf16[4,4,343,96]{2,3,1,0:T(8,128)(2,1)}, bf16[4,4,343,96]{2,3,1,0:T(8,128)(2,1)S(1)}, u32[]{:S(2)}) copy-start(bf16[4,4,343,96]{2,3,1,0:T(8,128)(2,1)S(1)} %get-tuple-element.421) | copy-start | bytes 3161092 | tf_op jit(solution)/shard_map/while
  304.4 6.9 slice-start
  328.7 9.3 %copy-start.9 = (bf16[4,4,343,96]{2,3,1,0:T(8,128)(2,1)}, bf16[4,4,343,96]{2,3,1,0:T(8,128)(2,1)S(1)}, u32[]{:S(2)}) copy-start(bf16[4,4,343,96]{2,3,1,0:T(8,128)(2,1)S(1)} %get-tuple-element.416) | copy-start | bytes 3161092 | tf_op jit(solution)/shard_map/while
  328.7 9.3 %copy-start.13 = (bf16[4,4,343,96]{2,3,1,0:T(8,128)(2,1)}, bf16[4,4,343,96]{2,3,1,0:T(8,128)(2,1)S(1)}, u32[]{:S(2)}) copy-start(bf16[4,4,343,96]{2,3,1,0:T(8,128)(2,1)S(1)} %get-tuple-element.421) | copy-start | bytes 3161092 | tf_op jit(solution)/shard_map/while
  338.3 6.9 slice-start
  367.1 81.4 %collective-permute-start.3 = (f32[3,28,7,96]{3,2,1,0:T(8,128)}, f32[3,28,7,96]{3,2,1,0:T(8,128)S(1)}, u32[]{:S(2)}, u32[]{:S(2)}) collective-permute-start(f32[3,28,7,96]{3,2,1,0:T(8,128)} %slice.79), channel_id=1, source_target_pairs={{24,0},{0,8},{8,16},{16,24},{25,1},{1,9},{9,17},{17,25},{26,2},{2,... | collective-permute-start | bytes 677384 | tf_op jit(solution)/shard_map/ppermute | solution.py:13
  388.9 59.6 %copy-start.4 = (f32[25,28,7,96]{3,2,1,0:T(8,128)S(1)}, f32[25,28,7,96]{3,2,1,0:T(8,128)}, u32[]{:S(2)}) copy-start(f32[25,28,7,96]{3,2,1,0:T(8,128)} %slice.80) | copy-start | bytes 5644804
  449.3 38.7 %collective-permute-start.4 = (f32[28,3,7,96]{3,2,1,0:T(8,128)}, f32[28,3,7,96]{3,2,1,0:T(8,128)}, u32[]{:S(2)}, u32[]{:S(2)}) collective-permute-start(f32[28,3,7,96]{3,2,1,0:T(8,128)} %pad_maximum_fusion.4), channel_id=1, source_target_pairs={{6,0},{0,2},{2,4},{4,6},{7,1},{1,3},{3,5},{5,7},{14,8},{8,10},{10,... | collective-permute-start | bytes 677384 | tf_op jit(solution)/shard_map/ppermute | solution.py:13
  489.6 8.8 %copy-start.15 = (f32[28,28,7,96]{3,2,1,0:T(8,128)}, f32[28,28,7,96]{3,2,1,0:T(8,128)S(1)}, u32[]{:S(2)}) copy-start(f32[28,28,7,96]{3,2,1,0:T(8,128)S(1)} %fusion.63) | copy-start | bytes 6322180
  491.3 135.1 %collective-permute-start.5 = (f32[28,28,3,96]{3,1,2,0:T(8,128)}, f32[28,28,3,96]{3,1,2,0:T(8,128)S(1)}, u32[]{:S(2)}, u32[]{:S(2)}) collective-permute-start(f32[28,28,3,96]{3,1,2,0:T(8,128)} %copy.86), channel_id=1, source_target_pairs={{1,0},{0,1},{3,2},{2,3},{5,4},{4,5},{7,6},{6,7},{9,8},{8,9},{11,10... | collective-permute-start | bytes 2709512 | tf_op jit(solution)/shard_map/ppermute | solution.py:13
  628.2 54.6 %copy-start.6 = (bf16[28,28,7,96]{3,2,1,0:T(8,128)(2,1)S(1)}, bf16[28,28,7,96]{3,2,1,0:T(8,128)(2,1)}, u32[]{:S(2)}) copy-start(bf16[28,28,7,96]{3,2,1,0:T(8,128)(2,1)} %param.11) | copy-start | bytes 3161092
  (31 other events, 133.9 us)
Sparse Core Ops, SparseCore 0:
  498.6 122.2 all-reduce.2
where the time goes:
time: 706 us; the launch traced here: 698 us
  matrix products  211 us (30%)
  local copies, waits for them, and re-layouts  203 us (29%)
  waiting for transfers between devices  125 us (18%)
  other arithmetic  73.7 us (10%)
  blocking collectives  43.7 us (6%)
  starting transfers between devices  26.1 us (4%)
  between operations  14.7 us (2%)
    psum x1, waiting for transfers between devices, shards(): lax.psum((sums[0], sums[1], sums[2], rel_local, local_gain, shift_local),...  121 us
    reshape x2, local copies, waits for them, and re-layouts, fold_table(): grid = pairs.reshape(heads, span, span, span, span, span, span)  79.7 us
    dot_general x1, matrix products, expand_table(): section = jnp.einsum('hxbcBC,aAx->habcABC', section, ones, precision=exact)  71.1 us
    unnamed x51, local copies, waits for them, and re-layouts  67.5 us
    psum x1, blocking collectives, shards(): lax.psum((sums[0], sums[1], sums[2], rel_local, local_gain, shift_local),...  43.7 us
    sub x4, matrix products, window_pass(): expo = jnp.exp(scores - top)  27.8 us
    dot_general x4, matrix products, window_pass(): jnp.einsum('ghid,ghjd->ghij', grad_heads, values, preferred_element_type=...  27.7 us
    ppermute x6, starting transfers between devices, shifted(): return lax.ppermute(block, axis, route)  26 us
  transfers between devices with their start and end apart: 7, of which 2 were waited for; matrix products, arithmetic and copies ran while one was open for 43% of the time, Pallas kernels for 0%

commit v1 on v0

--- a/solution.py
+++ b/solution.py
@@ -196,9 +196,9 @@
     rel_local = fold_table(sums[3], WIN)
     local_gain = jnp.sum(normalized_output_gradient * normalized_input, (0, 1, 2))
     shift_local = jnp.sum(normalized_output_gradient, (0, 1, 2))
-    totals = lax.psum(
-        (sums[0], sums[1], sums[2], rel_local, local_gain, shift_local), ("gx", "gy", "gz")
-    )
+    totals = (sums[0], sums[1], sums[2], rel_local, local_gain, shift_local)
+    for mesh_axis in (("gy", "gz"), "gx"):
+        totals = lax.psum(totals, mesh_axis)
     count = (
         cells_x
         * cells_y

time: 706 us -> 664 us (0.941)
  waiting for transfers between devices: 125 us -> 81.8 us
    psum x1 -> x2, waiting for transfers between devices: 121 us -> 77.8 us  [shards(): totals = lax.psum(totals, mesh_axis)]
    psum x1 -> x2, blocking collectives: 43.7 us -> 44.8 us  [shards(): totals = lax.psum(totals, mesh_axis)]
  transfers between devices with their start and end apart: 7 -> 8, of which waited for: 2 -> 3; matrix products, arithmetic and copies ran while one was open for 43% -> 46% of each run, Pallas kernels for 0% -> 0%
where the time goes in v1:
time: 664 us; the launch traced here: 656 us
  matrix products  210 us (32%)
  local copies, waits for them, and re-layouts  204 us (31%)
  waiting for transfers between devices  81.8 us (12%)
  other arithmetic  73.7 us (11%)
  blocking collectives  44.8 us (7%)
  starting transfers between devices  26.3 us (4%)
  between operations  14.8 us (2%)
    reshape x2, local copies, waits for them, and re-layouts, fold_table(): grid = pairs.reshape(heads, span, span, span, span, span, span)  79.8 us
    psum x2, waiting for transfers between devices, shards(): totals = lax.psum(totals, mesh_axis)  77.8 us
    dot_general x1, matrix products, expand_table(): section = jnp.einsum('hxbcBC,aAx->habcABC', section, ones, precision=exact)  71.1 us
    unnamed x51, local copies, waits for them, and re-layouts  68.1 us
    psum x2, blocking collectives, shards(): totals = lax.psum(totals, mesh_axis)  44.8 us
    sub x4, matrix products, window_pass(): expo = jnp.exp(scores - top)  27.7 us
    dot_general x4, matrix products, window_pass(): jnp.einsum('ghid,ghjd->ghij', grad_heads, values, preferred_element_type=...  27.6 us
    ppermute x6, starting transfers between devices, shifted(): return lax.ppermute(block, axis, route)  26 us
  transfers between devices with their start and end apart: 8, of which 3 were waited for; matrix products, arithmetic and copies ran while one was open for 46% of the time, Pallas kernels for 0%

profile of v1, /device:TPU:0, one launch (start us, length us, event | category | flops | bytes accessed | tf_op | source)
XLA Modules:
  0.0 656.2 jit_solution(4956379097109403098)
XLA Ops:
  21.9 9.5 %convolution_bitcast_fusion.5 = f32[3,13,7,7,7,7]{1,2,5,3,0,4:T(8,128)S(1)} fusion(f32[3,13,13,7,7]{2,3,1,0,4:T(8,128)S(1)} %convolution_bitcast_fusion.7, s32[7,7]{0,1:T(8,128)S(1)} %subtract_add_fusion), kind=kOutput, calls=%fused_computation.96 | convolution fusion | flops 14608321 | bytes 474124 | tf_op jit(solution)/shard_map/hxycC,bBy->hxbcBC/dot_general | solution.py:30
  32.4 18.0 %collective-permute-start.1 = (bf16[2,28,3,7,96]{4,3,2,1,0:T(8,128)(2,1)S(1)}, bf16[2,28,3,7,96]{4,3,2,1,0:T(8,128)(2,1)S(1)}, u32[]{:S(2)}, u32[]{:S(2)}) collective-permute-start(bf16[2,28,3,7,96]{4,3,2,1,0:T(8,128)(2,1)S(1)} %pad_maximum_fusion.5), channel_id=1, source_target_pairs={{2,0},{4,2},{6,4},{0,6},{3,1},{5,3},{7,5},{1,7},{10,8},{12,10},{14... | collective-permute-start | bytes 677384 | tf_op jit(solution)/shard_map/ppermute | solution.py:13
  60.5 71.1 %convolution_bitcast_fusion.3 = f32[3,7,7,7,7,7,7]{6,4,5,3,2,0,1:T(8,128)} fusion(f32[3,13,7,7,7,7]{1,2,5,3,0,4:T(8,128)S(1)} %convolution_bitcast_fusion.5, pred[7,7,13,1,1,1,1]{2,0,1,6,5,4,3:T(8,128)(4,1)S(1)} %fusion.73), kind=kOutput, calls=%fused_computation.61 | convolution fusion | flops 55059736 | bytes 1786981 | tf_op jit(solution)/shard_map/hxbcBC,aAx->habcABC/dot_general | solution.py:31
  131.6 59.5 %copy.82 = f32[3,7,7,7,7,7,7]{3,2,1,6,5,4,0:T(8,128)} copy(f32[3,7,7,7,7,7,7]{6,4,5,3,2,0,1:T(8,128)} %convolution_bitcast_fusion.3) | data formatting | bytes 2823576
  191.2 20.9 %add.252 = f32[3,343,343]{1,2,0:T(8,128)} reshape(f32[3,7,7,7,7,7,7]{3,2,1,6,5,4,0:T(8,128)} %copy.82) | data formatting | bytes 2823576 | tf_op jit(solution)/shard_map/while/body/eval_jaxpr/add | solution.py:113
  228.5 133.8 %while.20 = (s32[]{:T(128)}, f32[96,288]{1,0:T(8,128)}, f32[288]{0:T(512)S(1)}, f32[96,96]{1,0:T(8,128)S(1)}, f32[3,343,343]{1,2,0:T(8,128)}, /*index=5*/f32[4,4...) while((s32[]{:T(128)}, f32[96,288]{1,0:T(8,128)}, ...), condition=%wide.wide.region_8.9_spmd.clone, body=%wide.wide.region_2.8_spmd.clone.sunk | while | flops 848489408 | bytes 107633568 | solution.py:183
  231.1 6.9 %fusion.174 = (f32[4,3,343]{2,1,0:T(4,128)S(1)}, f32[4,3,343,343]{2,3,1,0:T(8,128)}) fusion(f32[3,343,343]{1,2,0:T(8,128)} %get-tuple-element.428, pred[4,343,343]{1,2,0:T(8,128)(4,1)} %broadcast_compare_fusion.3, bf16[4,343,3,3,32]{1,4,3,2,0:T(8,128)(2,1)S(1)} %bitcast.281), kind=kOutput, calls=%fused_computation.146.clone.clone.1 | convolution fusion | flops 97413720 | bytes 8135824 | tf_op jit(solution)/shard_map/while/body/eval_jaxpr/sub | solution.py:119
  238.2 6.9 %multiply_reduce_fusion.4 = (f32[4,3,343]{2,1,0:T(4,128)S(1)}, f32[4,3,343,343]{2,3,1,0:T(8,128)}) fusion(f32[4,3,343,343]{2,3,1,0:T(8,128)} %get-tuple-element.377, f32[4,3,343]{2,1,0:T(4,128)S(1)} %get-tuple-element.378, bf16[4,3,343,32]{2,3,1,0:T(8,128)(2,1)S(1)} %bitcast.292, bf16[4,343,3,3,32]{1,4,3,2,0:T(8,128)(2,1)S(1)} %bitcast.282), kind=kOutput, calls=%fused_computation.2.clone.clone.1 | convolution fusion | flops 94585688 | bytes 11925168 | tf_op jit(solution)/shard_map/while/body/eval_jaxpr/ghid,ghjd->ghij/dot_general | solution.py:127
  263.3 6.9 %fusion.174 = (f32[4,3,343]{2,1,0:T(4,128)S(1)}, f32[4,3,343,343]{2,3,1,0:T(8,128)}) fusion(f32[3,343,343]{1,2,0:T(8,128)} %get-tuple-element.428, pred[4,343,343]{1,2,0:T(8,128)(4,1)} %broadcast_compare_fusion.3, bf16[4,343,3,3,32]{1,4,3,2,0:T(8,128)(2,1)S(1)} %bitcast.281), kind=kOutput, calls=%fused_computation.146.clone.clone.1 | convolution fusion | flops 97413720 | bytes 8135824 | tf_op jit(solution)/shard_map/while/body/eval_jaxpr/sub | solution.py:119
  270.6 6.9 %multiply_reduce_fusion.4 = (f32[4,3,343]{2,1,0:T(4,128)S(1)}, f32[4,3,343,343]{2,3,1,0:T(8,128)}) fusion(f32[4,3,343,343]{2,3,1,0:T(8,128)} %get-tuple-element.377, f32[4,3,343]{2,1,0:T(4,128)S(1)} %get-tuple-element.378, bf16[4,3,343,32]{2,3,1,0:T(8,128)(2,1)S(1)} %bitcast.292, bf16[4,343,3,3,32]{1,4,3,2,0:T(8,128)(2,1)S(1)} %bitcast.282), kind=kOutput, calls=%fused_computation.2.clone.clone.1 | convolution fusion | flops 94585688 | bytes 11925168 | tf_op jit(solution)/shard_map/while/body/eval_jaxpr/ghid,ghjd->ghij/dot_general | solution.py:127
  297.1 6.9 %fusion.174 = (f32[4,3,343]{2,1,0:T(4,128)S(1)}, f32[4,3,343,343]{2,3,1,0:T(8,128)}) fusion(f32[3,343,343]{1,2,0:T(8,128)} %get-tuple-element.428, pred[4,343,343]{1,2,0:T(8,128)(4,1)} %broadcast_compare_fusion.3, bf16[4,343,3,3,32]{1,4,3,2,0:T(8,128)(2,1)S(1)} %bitcast.281), kind=kOutput, calls=%fused_computation.146.clone.clone.1 | convolution fusion | flops 97413720 | bytes 8135824 | tf_op jit(solution)/shard_map/while/body/eval_jaxpr/sub | solution.py:119
  304.3 6.9 %multiply_reduce_fusion.4 = (f32[4,3,343]{2,1,0:T(4,128)S(1)}, f32[4,3,343,343]{2,3,1,0:T(8,128)}) fusion(f32[4,3,343,343]{2,3,1,0:T(8,128)} %get-tuple-element.377, f32[4,3,343]{2,1,0:T(4,128)S(1)} %get-tuple-element.378, bf16[4,3,343,32]{2,3,1,0:T(8,128)(2,1)S(1)} %bitcast.292, bf16[4,343,3,3,32]{1,4,3,2,0:T(8,128)(2,1)S(1)} %bitcast.282), kind=kOutput, calls=%fused_computation.2.clone.clone.1 | convolution fusion | flops 94585688 | bytes 11925168 | tf_op jit(solution)/shard_map/while/body/eval_jaxpr/ghid,ghjd->ghij/dot_general | solution.py:127
  330.9 6.9 %fusion.174 = (f32[4,3,343]{2,1,0:T(4,128)S(1)}, f32[4,3,343,343]{2,3,1,0:T(8,128)}) fusion(f32[3,343,343]{1,2,0:T(8,128)} %get-tuple-element.428, pred[4,343,343]{1,2,0:T(8,128)(4,1)} %broadcast_compare_fusion.3, bf16[4,343,3,3,32]{1,4,3,2,0:T(8,128)(2,1)S(1)} %bitcast.281), kind=kOutput, calls=%fused_computation.146.clone.clone.1 | convolution fusion | flops 97413720 | bytes 8135824 | tf_op jit(solution)/shard_map/while/body/eval_jaxpr/sub | solution.py:119
  338.1 6.9 %multiply_reduce_fusion.4 = (f32[4,3,343]{2,1,0:T(4,128)S(1)}, f32[4,3,343,343]{2,3,1,0:T(8,128)}) fusion(f32[4,3,343,343]{2,3,1,0:T(8,128)} %get-tuple-element.377, f32[4,3,343]{2,1,0:T(4,128)S(1)} %get-tuple-element.378, bf16[4,3,343,32]{2,3,1,0:T(8,128)(2,1)S(1)} %bitcast.292, bf16[4,343,3,3,32]{1,4,3,2,0:T(8,128)(2,1)S(1)} %bitcast.282), kind=kOutput, calls=%fused_computation.2.clone.clone.1 | convolution fusion | flops 94585688 | bytes 11925168 | tf_op jit(solution)/shard_map/while/body/eval_jaxpr/ghid,ghjd->ghij/dot_general | solution.py:127
  368.7 20.1 %reshape.160 = f32[3,7,7,7,7,7,7]{3,2,1,6,5,4,0:T(8,128)} reshape(f32[3,343,343]{1,2,0:T(8,128)S(1)} %copy-done) | data formatting | bytes 2823576 | tf_op jit(solution)/shard_map/reshape | solution.py:39
  388.7 59.7 %copy.88 = f32[3,7,7,7,7,7,7]{1,6,4,5,3,2,0:T(8,128)} copy(f32[3,7,7,7,7,7,7]{3,2,1,6,5,4,0:T(8,128)} %reshape.160) | data formatting | bytes 2823576 | tf_op jit(solution)/shard_map/reshape | solution.py:39
  450.1 25.0 %convolution_bitcast_fusion.4 = f32[3,13,7,7,7,7]{1,5,4,3,2,0:T(8,128)} fusion(f32[3,7,7,7,7,7,7]{1,6,4,5,3,2,0:T(8,128)} %copy.88, s32[7,7]{0,1:T(8,128)S(1)} %copy-done.22), kind=kOutput, calls=%fused_computation.95 | convolution fusion | flops 55060372 | bytes 1786540 | tf_op jit(solution)/shard_map/habcABC,aAx->hxbcBC/dot_general | solution.py:40
  475.1 12.7 %copy.89 = f32[3,13,7,7,7,7]{2,3,4,5,1,0:T(8,128)} copy(f32[3,13,7,7,7,7]{1,5,4,3,2,0:T(8,128)} %convolution_bitcast_fusion.4) | data formatting | bytes 749112 | tf_op jit(solution)/shard_map/habcABC,aAx->hxbcBC/transpose | solution.py:40
  499.0 41.5 %all-reduce.5.cloned.1.call-done = f32[96,288]{1,0:T(8,128)} async-done(((f32[96,288]{1,0:T(8,128)}), f32[96,288]{1,0:T(8,128)}) %all-reduce.5.cloned.1.call-update) | async-done | bytes 110608 | tf_op jit(solution)/shard_map/psum | solution.py:201
  541.8 36.3 %all-reduce.7.cloned.1.call-done = f32[96,288]{1,0:T(8,128)} async-done(((f32[96,288]{1,0:T(8,128)}), f32[96,288]{1,0:T(8,128)}) %all-reduce.7.cloned.1.call-update) | async-done | bytes 110608 | tf_op jit(solution)/shard_map/psum | solution.py:201
  585.4 5.9 fusion.61
  591.4 25.5 %all-reduce = (f32[288]{0:T(512)S(1)}, f32[96,96]{1,0:T(8,128)S(1)}, f32[3,2197]{1,0:T(4,128)S(1)}, f32[96]{0:T(128)S(1)}, f32[96]{0:T(128)S(1)}) all-reduce(f32[288]{0:T(512)S(1)} %get-tuple-element.80, f32[96,96]{1,0:T(8,128)S(1)} %get-tuple-element.81, ...), channel_id=1, replica_groups=mesh['gx'=4,'gy'=4,'gz'=2] {'gy','gz'}, use_global_device_ids=true, to_apply=%region_13.14 | all-reduce | flops 16287 | bytes 130296 | tf_op jit(solution)/shard_map/psum | solution.py:201
  616.9 19.3 %all-reduce.1 = (f32[288]{0:T(512)S(1)}, f32[96,96]{1,0:T(8,128)S(1)}, f32[3,2197]{1,0:T(4,128)S(1)}, f32[96]{0:T(128)S(1)}, f32[96]{0:T(128)S(1)}) all-reduce(f32[288]{0:T(512)S(1)} %get-tuple-element.206, f32[96,96]{1,0:T(8,128)S(1)} %get-tuple-element.207, ...), channel_id=1, replica_groups=mesh['gx'=4,'gy'=4,'gz'=2] {'gx'}, use_global_device_ids=true, to_apply=%region_14.15 | all-reduce | flops 16287 | bytes 130296 | tf_op jit(solution)/shard_map/psum | solution.py:201
  641.2 8.0 %fusion.60 = bf16[28,28,7,96]{3,2,1,0:T(8,128)(2,1)} fusion(bf16[28,28,7,96]{3,2,1,0:T(8,128)(2,1)S(1)} %copy-done.2, bf16[28,28,7,96]{3,2,1,0:T(8,128)(2,1)S(1)} %copy-done.6, f32[28,28,7]{2,1,0:T(8,128)S(1)} %broadcast_multiply_fusion, f32[28,28,7]{2,1,0:T(8,128)S(1)} %broadcast_multiply_fusion.1, f32[96]{0:T(128)S(1)} %copy-done.26, ...), kind=kLoop, calls=%fused_computation.78 | loop fusion | flops 6322176 | bytes 5356672 | tf_op jit(solution)/shard_map/convert_element_type | solution.py:195
  (242 shorter events, 152.1 us)
Async XLA Ops:
  7.2 533.3 %all-reduce.5.cloned.1.call-start = ((), (), s32[]{:S(2)}) async-start(), calls=%async_computation | async-start | bytes 294912 | tf_op jit(solution)/shard_map/psum | solution.py:201
  15.1 17.2 %collective-permute-start = (bf16[2,3,28,7,96]{4,3,2,1,0:T(8,128)(2,1)S(1)}, bf16[2,3,28,7,96]{4,3,2,1,0:T(8,128)(2,1)S(1)}, u32[]{:S(2)}, u32[]{:S(2)}) collective-permute-start(bf16[2,3,28,7,96]{4,3,2,1,0:T(8,128)(2,1)S(1)} %pad_maximum_fusion.6), channel_id=1, source_target_pairs={{8,0},{16,8},{24,16},{0,24},{9,1},{17,9},{25,17},{1,25},{10,2},{18... | collective-permute-start | bytes 677384 | tf_op jit(solution)/shard_map/ppermute | solution.py:13
  20.2 30.2 %copy-start.21 = (s32[7,7]{0,1:T(8,128)}, s32[7,7]{0,1:T(8,128)S(1)}, u32[]{:S(2)}) copy-start(s32[7,7]{0,1:T(8,128)S(1)} %subtract_add_fusion) | copy-start | bytes 592
  20.5 11.0 %copy-start.12 = (bf16[1,28,28,7,96]{4,3,2,1,0:T(8,128)(2,1)S(1)}, bf16[1,28,28,7,96]{4,3,2,1,0:T(8,128)(2,1)}, u32[]{:S(2)}) copy-start(bf16[1,28,28,7,96]{4,3,2,1,0:T(8,128)(2,1)} %copy-done.11) | copy-start | bytes 3161092
  32.4 22.8 %collective-permute-start.1 = (bf16[2,28,3,7,96]{4,3,2,1,0:T(8,128)(2,1)S(1)}, bf16[2,28,3,7,96]{4,3,2,1,0:T(8,128)(2,1)S(1)}, u32[]{:S(2)}, u32[]{:S(2)}) collective-permute-start(bf16[2,28,3,7,96]{4,3,2,1,0:T(8,128)(2,1)S(1)} %pad_maximum_fusion.5), channel_id=1, source_target_pairs={{2,0},{4,2},{6,4},{0,6},{3,1},{5,3},{7,5},{1,7},{10,8},{12,10},{14... | collective-permute-start | bytes 677384 | tf_op jit(solution)/shard_map/ppermute | solution.py:13
  59.0 156.9 %collective-permute-start.2 = (bf16[2,28,28,3,96]{4,0,3,2,1:T(2,128)(2,1)}, bf16[2,28,28,3,96]{4,0,3,2,1:T(2,128)(2,1)}, u32[]{:S(2)}, u32[]{:S(2)}) collective-permute-start(bf16[2,28,28,3,96]{4,0,3,2,1:T(2,128)(2,1)} %copy.74), channel_id=1, source_target_pairs={{1,0},{0,1},{3,2},{2,3},{5,4},{4,5},{7,6},{6,7},{9,8},{8,9},{11,10... | collective-permute-start | bytes 2709512 | tf_op jit(solution)/shard_map/ppermute | solution.py:13
  228.7 9.3 %copy-start.9 = (bf16[4,4,343,96]{2,3,1,0:T(8,128)(2,1)}, bf16[4,4,343,96]{2,3,1,0:T(8,128)(2,1)S(1)}, u32[]{:S(2)}) copy-start(bf16[4,4,343,96]{2,3,1,0:T(8,128)(2,1)S(1)} %get-tuple-element.421) | copy-start | bytes 3161092 | tf_op jit(solution)/shard_map/while
  228.7 9.3 %copy-start.13 = (bf16[4,4,343,96]{2,3,1,0:T(8,128)(2,1)}, bf16[4,4,343,96]{2,3,1,0:T(8,128)(2,1)S(1)}, u32[]{:S(2)}) copy-start(bf16[4,4,343,96]{2,3,1,0:T(8,128)(2,1)S(1)} %get-tuple-element.426) | copy-start | bytes 3161092 | tf_op jit(solution)/shard_map/while
  238.2 6.9 %slice-start = ((s8[6340608]{0:T(1024)(128)(4,1)}), s8[4194304]{0:T(1024)(128)(4,1)S(1)}, s32[]{:S(2)}) async-start(s8[6340608]{0:T(1024)(128)(4,1)} %bitcast.279), calls=%async_computation.2 | async-start | bytes 8388608 | tf_op jit(solution)/shard_map/while
  261.0 9.3 %copy-start.9 = (bf16[4,4,343,96]{2,3,1,0:T(8,128)(2,1)}, bf16[4,4,343,96]{2,3,1,0:T(8,128)(2,1)S(1)}, u32[]{:S(2)}) copy-start(bf16[4,4,343,96]{2,3,1,0:T(8,128)(2,1)S(1)} %get-tuple-element.421) | copy-start | bytes 3161092 | tf_op jit(solution)/shard_map/while
  261.0 9.3 %copy-start.13 = (bf16[4,4,343,96]{2,3,1,0:T(8,128)(2,1)}, bf16[4,4,343,96]{2,3,1,0:T(8,128)(2,1)S(1)}, u32[]{:S(2)}) copy-start(bf16[4,4,343,96]{2,3,1,0:T(8,128)(2,1)S(1)} %get-tuple-element.426) | copy-start | bytes 3161092 | tf_op jit(solution)/shard_map/while
  270.5 6.9 %slice-start = ((s8[6340608]{0:T(1024)(128)(4,1)}), s8[4194304]{0:T(1024)(128)(4,1)S(1)}, s32[]{:S(2)}) async-start(s8[6340608]{0:T(1024)(128)(4,1)} %bitcast.279), calls=%async_computation.2 | async-start | bytes 8388608 | tf_op jit(solution)/shard_map/while
  294.8 9.3 %copy-start.9 = (bf16[4,4,343,96]{2,3,1,0:T(8,128)(2,1)}, bf16[4,4,343,96]{2,3,1,0:T(8,128)(2,1)S(1)}, u32[]{:S(2)}) copy-start(bf16[4,4,343,96]{2,3,1,0:T(8,128)(2,1)S(1)} %get-tuple-element.421) | copy-start | bytes 3161092 | tf_op jit(solution)/shard_map/while
  294.8 9.3 %copy-start.13 = (bf16[4,4,343,96]{2,3,1,0:T(8,128)(2,1)}, bf16[4,4,343,96]{2,3,1,0:T(8,128)(2,1)S(1)}, u32[]{:S(2)}) copy-start(bf16[4,4,343,96]{2,3,1,0:T(8,128)(2,1)S(1)} %get-tuple-element.426) | copy-start | bytes 3161092 | tf_op jit(solution)/shard_map/while
  304.3 6.9 %slice-start = ((s8[6340608]{0:T(1024)(128)(4,1)}), s8[4194304]{0:T(1024)(128)(4,1)S(1)}, s32[]{:S(2)}) async-start(s8[6340608]{0:T(1024)(128)(4,1)} %bitcast.279), calls=%async_computation.2 | async-start | bytes 8388608 | tf_op jit(solution)/shard_map/while
  328.5 9.3 %copy-start.9 = (bf16[4,4,343,96]{2,3,1,0:T(8,128)(2,1)}, bf16[4,4,343,96]{2,3,1,0:T(8,128)(2,1)S(1)}, u32[]{:S(2)}) copy-start(bf16[4,4,343,96]{2,3,1,0:T(8,128)(2,1)S(1)} %get-tuple-element.421) | copy-start | bytes 3161092 | tf_op jit(solution)/shard_map/while
  328.5 9.3 %copy-start.13 = (bf16[4,4,343,96]{2,3,1,0:T(8,128)(2,1)}, bf16[4,4,343,96]{2,3,1,0:T(8,128)(2,1)S(1)}, u32[]{:S(2)}) copy-start(bf16[4,4,343,96]{2,3,1,0:T(8,128)(2,1)S(1)} %get-tuple-element.426) | copy-start | bytes 3161092 | tf_op jit(solution)/shard_map/while
  338.1 6.9 %slice-start = ((s8[6340608]{0:T(1024)(128)(4,1)}), s8[4194304]{0:T(1024)(128)(4,1)S(1)}, s32[]{:S(2)}) async-start(s8[6340608]{0:T(1024)(128)(4,1)} %bitcast.279), calls=%async_computation.2 | async-start | bytes 8388608 | tf_op jit(solution)/shard_map/while
  366.9 81.6 %collective-permute-start.3 = (f32[3,28,7,96]{3,2,1,0:T(8,128)}, f32[3,28,7,96]{3,2,1,0:T(8,128)S(1)}, u32[]{:S(2)}, u32[]{:S(2)}) collective-permute-start(f32[3,28,7,96]{3,2,1,0:T(8,128)} %slice.79), channel_id=1, source_target_pairs={{24,0},{0,8},{8,16},{16,24},{25,1},{1,9},{9,17},{17,25},{26,2},{2,... | collective-permute-start | bytes 677384 | tf_op jit(solution)/shard_map/ppermute | solution.py:13
  388.7 59.7 %copy-start.4 = (f32[25,28,7,96]{3,2,1,0:T(8,128)S(1)}, f32[25,28,7,96]{3,2,1,0:T(8,128)}, u32[]{:S(2)}) copy-start(f32[25,28,7,96]{3,2,1,0:T(8,128)} %slice.80) | copy-start | bytes 5644804
  449.2 38.8 %collective-permute-start.4 = (f32[28,3,7,96]{3,2,1,0:T(8,128)}, f32[28,3,7,96]{3,2,1,0:T(8,128)}, u32[]{:S(2)}, u32[]{:S(2)}) collective-permute-start(f32[28,3,7,96]{3,2,1,0:T(8,128)} %pad_maximum_fusion.4), channel_id=1, source_target_pairs={{6,0},{0,2},{2,4},{4,6},{7,1},{1,3},{3,5},{5,7},{14,8},{8,10},{10,... | collective-permute-start | bytes 677384 | tf_op jit(solution)/shard_map/ppermute | solution.py:13
  487.8 90.3 %all-reduce.7.cloned.1.call-start = ((), (), s32[]{:S(2)}) async-start(), calls=%async_computation.1 | async-start | bytes 294912 | tf_op jit(solution)/shard_map/psum | solution.py:201
  493.1 90.6 %collective-permute-start.5 = (f32[28,28,3,96]{3,1,2,0:T(8,128)}, f32[28,28,3,96]{3,1,2,0:T(8,128)S(1)}, u32[]{:S(2)}, u32[]{:S(2)}) collective-permute-start(f32[28,28,3,96]{3,1,2,0:T(8,128)} %copy.86), channel_id=1, source_target_pairs={{1,0},{0,1},{3,2},{2,3},{5,4},{4,5},{7,6},{6,7},{9,8},{8,9},{11,10... | collective-permute-start | bytes 2709512 | tf_op jit(solution)/shard_map/ppermute | solution.py:13
  585.4 55.7 %copy-start.6 = (bf16[28,28,7,96]{3,2,1,0:T(8,128)(2,1)S(1)}, bf16[28,28,7,96]{3,2,1,0:T(8,128)(2,1)}, u32[]{:S(2)}) copy-start(bf16[28,28,7,96]{3,2,1,0:T(8,128)(2,1)} %param.11) | copy-start | bytes 3161092
  (32 other events, 136.2 us)
Sparse Core Ops, SparseCore 0:
  487.9 52.5 all-reduce.4
  542.8 35.2 all-reduce.6
